TPU v7x, 32 devices: a whole 2x2x4 slice. The times are simulated.
32 devices in a mesh: date: 8 (over z, x), pix: 4 (over y, core).
Axes of the slice: x: 2, y: 2, z: 4, core: 2. Of those that a mesh axis runs over, the one named last changes fastest.
Arguments:
- stack: bfloat16 [8, 10, 32, 2048], P('date', None, 'pix'), may hold values from -4 to 12
- cloud: int32 [8, 32, 2048], P('date', 'pix'), may hold values 0 or 1
Outputs:
- composite: float32 [10, 32, 2048], P(None, 'pix')
All inputs are finite; a program needn't handle non-finite values. No bound on the sum of `cloud` on one device may be relied on, other than what follows from the above.
Results may differ from a plain program's by a relative error of at most 0.0003.
Values may be sent and summed in bfloat16 or wider, within the bound.
No kernel may reach another device: no remote copies, remote signals or barrier semaphores. Data moves between devices by JAX's collectives and lax.ppermute only.
A program may use at most 64 MiB of HBM per device.

v0:
```python
import jax
import jax.numpy as jnp
from jax import lax
from jax.sharding import PartitionSpec as P

ITERS = 2


delta_sq = 0.01
eps = 1e-05


def with_halo(cells, sides, width):
    for axis, dim in sides:
        count = lax.axis_size(axis)
        ends = count - 1
        head = lax.slice_in_dim(cells, 0, width, axis=dim)
        tail = lax.slice_in_dim(cells, cells.shape[dim] - width, cells.shape[dim], axis=dim)
        cells = jnp.concatenate(
            [
                lax.ppermute(tail, axis, [(i, (i + 1) % count) for i in range(ends)]),
                cells,
                lax.ppermute(head, axis, [((i + 1) % count, i) for i in range(ends)]),
            ],
            axis=dim,
        )
    return cells


def local_sums(values, valid, median, first):
    if first:
        weight = valid
    else:
        diff = values - median[None]
        weight = valid / jnp.sqrt(jnp.sum(diff * diff, axis=1) + delta_sq)
    numer = jnp.sum(weight[:, None] * values, axis=0)
    denom = jnp.sum(weight, axis=0, keepdims=True)
    return (numer, denom)


def moments(median):
    return (jnp.sum(median, axis=(1, 2)), jnp.sum(median * median, axis=(1, 2)))


def standardize(median, first_sum, second_sum, count):
    mean = first_sum / count
    var = second_sum / count - mean * mean
    return (median - mean[:, None, None]) / jnp.sqrt(var[:, None, None] + eps)


def body(stack, cloud):
    bands = stack.shape[1]
    rows = stack.shape[2]
    cols = stack.shape[3]
    cloudy = (1 - cloud).astype(jnp.bfloat16)
    rimmed = with_halo(cloudy, (("pix", 1),), 1).astype(jnp.float32)
    padded = jnp.pad(rimmed, ((0, 0), (0, 0), (1, 1)))
    near = jnp.maximum(padded[:, 1:-1, 1:-1], padded[:, 2:, 1:-1])
    near = jnp.maximum(near, padded[:, :-2, 1:-1])
    near = jnp.maximum(near, padded[:, 1:-1, 2:])
    near = jnp.maximum(near, padded[:, 1:-1, :-2])
    valid = 1.0 - near
    count = lax.axis_size("pix") * rows * cols
    values = stack.astype(jnp.float32)
    median = jnp.zeros((bands, rows, cols), jnp.float32)
    for step in range(ITERS + 1):
        numer, denom = local_sums(values, valid, median, step == 0)
        numer, denom = lax.psum((numer, denom), "date")
        median = (numer + median) / (denom + 1.0)
    first_sum, second_sum = moments(median)
    first_sum, second_sum = lax.psum((first_sum, second_sum), "pix")
    return standardize(median, first_sum, second_sum, count)


def solution(mesh):
    placed = (P("date", None, "pix", None), P("date", "pix", None))
    return jax.shard_map(
        body, mesh=mesh, in_specs=placed, out_specs=P(None, "pix", None), check_vma=False
    )
```

profile of v0, /device:TPU:0, one launch (start us, length us, event | category | flops | bytes accessed | tf_op | source)
XLA Modules:
  0.0 264.2 jit_solution(3385608217282337289)
XLA Ops:
  6.5 0.0 all-reduce.13.cloned.1.call-start
  6.5 0.8 subtract_convert_fusion
  7.4 2.4 collective-permute-start
  9.8 1.3 collective-permute-start.1
  11.1 0.0 collective-permute-done
  11.1 3.9 %collective-permute-done.1 = bf16[1,1,2048]{2,1,0:T(2,128)(2,1)S(1)} collective-permute-done((bf16[1,1,2048]{2,1,0:T(2,128)(2,1)S(1)}, bf16[1,1,2048]{2,1,0:T(2,128)(2,1)S(1)}, u32[]{:S(2)}, u32[]{:S(2)}) %collective-permute-start.1) | collective-permute-done | bytes 4128 | tf_op jit(solution)/shard_map/ppermute | solution.py:23
  15.0 0.0 copy-start
  15.0 0.1 fusion.12
  15.2 0.7 fusion.9
  15.9 0.1 copy-done
  16.0 0.9 fusion
  16.9 0.0 all-reduce.13.cloned.1.call-update
  16.9 0.0 all-reduce.11.cloned.1.call-start
  17.0 77.1 %all-reduce.13.cloned.1.call-done = (f32[10,8,2048]{2,1,0:T(8,128)}, f32[1,8,2048]{2,1,0:T(8,128)}) async-done(((f32[10,8,2048]{2,1,0:T(8,128)}, f32[1,8,2048]{2,1,0:T(8,128)}), (f32[10,8,2048]{2,1,0:T(8,128)}, f32[1,8,2048]{2,1,0:T(8,128)})) %all-reduce.13.cloned.1.call-update) | async-done | bytes 720912 | tf_op jit(solution)/shard_map/psum | solution.py:68
  94.1 0.8 add_bitcast_fusion.2
  94.9 1.2 fusion.2
  96.1 0.1 bitcast_multiply_fusion.1
  96.2 0.0 copy-start.2
  96.3 0.9 fusion.3
  97.1 0.0 copy-done.2
  97.2 0.0 copy-start.1
  97.2 0.0 all-reduce.11.cloned.1.call-update
  97.2 0.0 all-reduce.9.cloned.1.call-start
  97.2 74.3 %all-reduce.11.cloned.1.call-done = (f32[10,8,2048]{2,1,0:T(8,128)}, f32[1,8,2048]{2,1,0:T(8,128)}) async-done(((f32[10,8,2048]{2,1,0:T(8,128)}, f32[1,8,2048]{2,1,0:T(8,128)}), (f32[10,8,2048]{2,1,0:T(8,128)}, f32[1,8,2048]{2,1,0:T(8,128)})) %all-reduce.11.cloned.1.call-update) | async-done | bytes 720912 | tf_op jit(solution)/shard_map/psum | solution.py:68
  171.6 0.8 add_bitcast_fusion.1
  172.4 0.0 copy-done.1
  172.4 1.3 fusion.5
  173.7 0.1 bitcast_multiply_fusion
  173.8 0.0 copy-start.3
  173.8 0.9 fusion.6
  174.7 0.0 copy-done.3
  174.7 0.0 all-reduce.9.cloned.1.call-update
  174.7 74.2 %all-reduce.9.cloned.1.call-done = (f32[10,8,2048]{2,1,0:T(8,128)}, f32[1,8,2048]{2,1,0:T(8,128)}) async-done(((f32[10,8,2048]{2,1,0:T(8,128)}, f32[1,8,2048]{2,1,0:T(8,128)}), (f32[10,8,2048]{2,1,0:T(8,128)}, f32[1,8,2048]{2,1,0:T(8,128)})) %all-reduce.9.cloned.1.call-update) | async-done | bytes 720912 | tf_op jit(solution)/shard_map/psum | solution.py:68
  248.9 0.8 add_bitcast_fusion
  249.7 1.3 fusion.10
  251.1 5.7 %all-reduce.4 = (f32[10]{0:T(128)S(1)}, f32[10]{0:T(128)S(1)}) all-reduce(f32[10]{0:T(128)S(1)} %get-tuple-element.6, f32[10]{0:T(128)S(1)} %get-tuple-element.5), channel_id=1, replica_groups=mesh['date'=8,'pix'=4] {'pix'}, use_global_device_ids=true, to_apply=%region_11.12 | all-reduce | flops 20 | bytes 160 | tf_op jit(solution)/shard_map/psum | solution.py:71
  256.7 1.0 subtract_divide_fusion
  (3 shorter events, 0.1 us)
Async XLA Ops:
  6.5 87.5 %all-reduce.13.cloned.1.call-start = ((), (), s32[]{:S(2)}) async-start(), calls=%async_computation.2 | async-start | bytes 1441792 | tf_op jit(solution)/shard_map/psum | solution.py:68
  7.4 3.7 %collective-permute-start = (bf16[1,1,2048]{2,1,0:T(2,128)(2,1)S(1)}, bf16[1,1,2048]{2,1,0:T(2,128)(2,1)S(1)}, u32[]{:S(2)}, u32[]{:S(2)}) collective-permute-start(bf16[1,1,2048]{2,1,0:T(2,128)(2,1)S(1)} %get-tuple-element.18), channel_id=1, source_target_pairs={{0,1},{1,2},{2,3},{4,5},{5,6},{6,7},{8,9},{9,10},{10,11},{12,13},{... | collective-permute-start | bytes 12296 | tf_op jit(solution)/shard_map/ppermute | solution.py:21
  9.8 5.2 %collective-permute-start.1 = (bf16[1,1,2048]{2,1,0:T(2,128)(2,1)S(1)}, bf16[1,1,2048]{2,1,0:T(2,128)(2,1)S(1)}, u32[]{:S(2)}, u32[]{:S(2)}) collective-permute-start(bf16[1,1,2048]{2,1,0:T(2,128)(2,1)S(1)} %get-tuple-element.19), channel_id=1, source_target_pairs={{1,0},{2,1},{3,2},{5,4},{6,5},{7,6},{9,8},{10,9},{11,10},{13,12},{... | collective-permute-start | bytes 12296 | tf_op jit(solution)/shard_map/ppermute | solution.py:23
  15.0 1.0 copy-start
  16.9 154.6 %all-reduce.11.cloned.1.call-start = ((), (), s32[]{:S(2)}) async-start(), calls=%async_computation.1 | async-start | bytes 1441792 | tf_op jit(solution)/shard_map/psum | solution.py:68
  96.2 0.9 copy-start.2
  97.2 75.3 %copy-start.1 = (f32[10,8,2048]{2,1,0:T(8,128)S(1)}, f32[10,8,2048]{2,1,0:T(8,128)}, u32[]{:S(2)}) copy-start(f32[10,8,2048]{2,1,0:T(8,128)} %get-tuple-element.11) | copy-start | bytes 1966084
  97.2 151.7 %all-reduce.9.cloned.1.call-start = ((), (), s32[]{:S(2)}) async-start(), calls=%async_computation | async-start | bytes 1441792 | tf_op jit(solution)/shard_map/psum | solution.py:68
  173.8 0.9 copy-start.3
Sparse Core Ops, SparseCore 0:
  17.0 76.9 all-reduce.12
  97.6 73.8 all-reduce.10
  175.1 73.7 all-reduce.8
where the time goes:
time: 265 us; the launch traced here: 264 us
  waiting for transfers between devices  230 us (87%)
  between operations  13.2 us (5%)
  other arithmetic  11.9 us (4%)
  blocking collectives  5.65 us (2%)
  starting transfers between devices  3.77 us (1%)
    psum x3, waiting for transfers between devices, body(): numer, denom = lax.psum((numer, denom), 'date')  226 us
    psum x1, blocking collectives, body(): first_sum, second_sum = lax.psum((first_sum, second_sum), 'pix')  5.65 us
  transfers between devices with their start and end apart: 5, of which 4 were waited for; matrix products, arithmetic and copies ran while one was open for 0% of the time, Pallas kernels for 0%

commit v1 on v0

v1 whole, which is shorter than its diff:
```python
import jax
import jax.numpy as jnp
from jax import lax
from jax.sharding import PartitionSpec as P

ITERS = 2


delta_sq = 0.01
eps = 1e-05


def with_halo(cells, axis, dim):
    count = lax.axis_size(axis)
    ends = count - 1
    head = lax.slice_in_dim(cells, 0, 1, axis=dim)
    tail = lax.slice_in_dim(cells, cells.shape[dim] - 1, cells.shape[dim], axis=dim)
    return jnp.concatenate(
        [
            lax.ppermute(tail, axis, [(i, (i + 1) % count) for i in range(ends)]),
            cells,
            lax.ppermute(head, axis, [((i + 1) % count, i) for i in range(ends)]),
        ],
        axis=dim,
    )


def weiszfeld(values, valid):
    median = jnp.zeros(values.shape[1:], jnp.float32)
    for step in range(ITERS + 1):
        if step == 0:
            weight = valid
        else:
            diff = values - median[None]
            weight = valid / jnp.sqrt(jnp.sum(diff * diff, axis=1) + delta_sq)
        numer = jnp.sum(weight[:, None] * values, axis=0)
        denom = jnp.sum(weight, axis=0)
        median = (numer + median) / (denom + 1.0)
    return median


def body(stack, cloud):
    bands = stack.shape[1]
    rows = stack.shape[2]
    cols = stack.shape[3]
    cloudy = (1 - cloud).astype(jnp.bfloat16)
    rimmed = with_halo(cloudy, "pix", 1).astype(jnp.float32)
    padded = jnp.pad(rimmed, ((0, 0), (0, 0), (1, 1)))
    near = jnp.maximum(padded[:, 1:-1, 1:-1], padded[:, 2:, 1:-1])
    near = jnp.maximum(near, padded[:, :-2, 1:-1])
    near = jnp.maximum(near, padded[:, 1:-1, 2:])
    near = jnp.maximum(near, padded[:, 1:-1, :-2])
    valid = (1.0 - near).astype(jnp.bfloat16)
    planes = jnp.concatenate([stack, valid[:, None]], axis=1)
    planes = lax.all_to_all(planes, "date", 3, 0, tiled=True).astype(jnp.float32)
    median = weiszfeld(planes[:, :bands], planes[:, bands])
    median = lax.all_gather(median, "date", axis=2, tiled=True)
    count = lax.axis_size("pix") * rows * cols
    sums = lax.psum((jnp.sum(median, axis=(1, 2)), jnp.sum(median * median, axis=(1, 2))), "pix")
    mean = sums[0] / count
    var = sums[1] / count - mean * mean
    return (median - mean[:, None, None]) / jnp.sqrt(var[:, None, None] + eps)


def solution(mesh):
    placed = (P("date", None, "pix", None), P("date", "pix", None))
    return jax.shard_map(
        body, mesh=mesh, in_specs=placed, out_specs=P(None, "pix", None), check_vma=False
    )
```

time: 265 us -> 145 us (0.55)
  waiting for transfers between devices: 230 us -> 3.88 us
  blocking collectives: 5.65 us -> 54.1 us
  local copies, waits for them, and re-layouts: 0.16 us -> 46.4 us
  other arithmetic: 11.9 us -> 36.5 us
  between operations: 13.2 us -> 0.18 us
    psum x3 -> x0, waiting for transfers between devices: 226 us -> none  [body(): numer, denom = lax.psum((numer, denom), 'date')]
    all_gather x0 -> x1, blocking collectives: none -> 32 us  [body(): median = lax.all_gather(median, 'date', axis=2, tiled=True)]
    reduce_sum x6 -> x9, other arithmetic: 6.48 us -> 30.5 us  [the longest x3 14.6 us: weiszfeld(): numer = jnp.sum(weight[:, None] * values, axis=0)]
    unnamed x8, local copies, waits for them, and re-layouts: 0.14 us -> 17.5 us
    convert_element_type x0 -> x1, local copies, waits for them, and re-layouts: none -> 17.2 us  [body(): lax.all_to_all(planes, 'date', 3, 0, tiled=True).astype(jnp.float32)]
    all_to_all x0 -> x1, blocking collectives: none -> 16.5 us  [body(): lax.all_to_all(planes, 'date', 3, 0, tiled=True).astype(jnp.float32)]
    concatenate x0 -> x1, local copies, waits for them, and re-layouts: none -> 4.35 us  [body(): planes = jnp.concatenate([stack, valid[:, None]], axis=1)]
    reduce_sum x0 -> x3, local copies, waits for them, and re-layouts: none -> 3.86 us  [weiszfeld(): numer = jnp.sum(weight[:, None] * values, axis=0)]
  transfers between devices with their start and end apart: 5 -> 2, of which waited for: 4 -> 1; matrix products, arithmetic and copies ran while one was open for 0% -> 0% of each run, Pallas kernels for 0% -> 0%
where the time goes in v1:
time: 145 us
  blocking collectives  54.1 us (37%)
  local copies, waits for them, and re-layouts  46.4 us (32%)
  other arithmetic  36.5 us (25%)
  waiting for transfers between devices  3.88 us (3%)
  starting transfers between devices  3.69 us (3%)
    all_gather x1, blocking collectives, body(): median = lax.all_gather(median, 'date', axis=2, tiled=True)  32 us
    unnamed x8, local copies, waits for them, and re-layouts  17.5 us
    convert_element_type x1, local copies, waits for them, and re-layouts, body(): lax.all_to_all(planes, 'date', 3, 0, tiled=True).astype(jnp.float32)  17.2 us
    all_to_all x1, blocking collectives, body(): lax.all_to_all(planes, 'date', 3, 0, tiled=True).astype(jnp.float32)  16.5 us
    reduce_sum x3, other arithmetic, weiszfeld(): numer = jnp.sum(weight[:, None] * values, axis=0)  14.6 us
    reduce_sum x2, other arithmetic, weiszfeld(): weight = valid / jnp.sqrt(jnp.sum(diff * diff, axis=1) + delta_sq)  11.7 us
    psum x1, blocking collectives, body(): lax.psum((jnp.sum(median, axis=(1, 2)), jnp.sum(median * median, axis=(1,...  5.66 us
    concatenate x1, local copies, waits for them, and re-layouts, body(): planes = jnp.concatenate([stack, valid[:, None]], axis=1)  4.35 us
  transfers between devices with their start and end apart: 2, of which 1 were waited for; matrix products, arithmetic and copies ran while one was open for 0% of the time, Pallas kernels for 0%

profile of v1, /device:TPU:0, one launch (start us, length us, event | category | flops | bytes accessed | tf_op | source)
XLA Modules:
  0.0 144.7 jit_solution(4334048969689377763)
XLA Ops:
  0.0 0.8 subtract_convert_fusion
  0.9 2.4 %collective-permute-start = (bf16[1,1,2048]{2,1,0:T(2,128)(2,1)S(1)}, bf16[1,1,2048]{2,1,0:T(2,128)(2,1)S(1)}, u32[]{:S(2)}, u32[]{:S(2)}) collective-permute-start(bf16[1,1,2048]{2,1,0:T(2,128)(2,1)S(1)} %get-tuple-element.11), channel_id=1, source_target_pairs={{0,1},{1,2},{2,3},{4,5},{5,6},{6,7},{8,9},{9,10},{10,11},{12,13},{... | collective-permute-start | bytes 12296 | tf_op jit(solution)/shard_map/ppermute | solution.py:20
  3.3 1.3 collective-permute-start.1
  4.6 0.0 collective-permute-done
  4.6 3.9 %collective-permute-done.1 = bf16[1,1,2048]{2,1,0:T(2,128)(2,1)S(1)} collective-permute-done((bf16[1,1,2048]{2,1,0:T(2,128)(2,1)S(1)}, bf16[1,1,2048]{2,1,0:T(2,128)(2,1)S(1)}, u32[]{:S(2)}, u32[]{:S(2)}) %collective-permute-start.1) | collective-permute-done | bytes 4128 | tf_op jit(solution)/shard_map/ppermute | solution.py:22
  8.5 0.1 fusion.6
  8.6 1.0 pad_maximum_fusion
  9.6 4.3 %copy.33 = bf16[1,11,8,2048]{1,2,0,3:T(8,128)(2,1)} copy(bf16[1,11,8,2048]{3,2,1,0:T(8,128)(2,1)S(1)} %pad_maximum_fusion) | data formatting | bytes 720896 | tf_op jit(solution)/shard_map/concatenate | solution.py:54
  14.0 7.3 %reshape.94 = bf16[8,2,11264]{2,1,0:T(2,128)(2,1)S(1)} reshape(bf16[2048,1,8,11]{3,2,1,0:T(8,128)(2,1)} %bitcast.38) | data formatting | bytes 720896
  21.2 16.5 %all_to_all.4 = bf16[8,2,11264]{2,1,0:T(2,128)(2,1)S(1)} all-to-all(bf16[8,2,11264]{2,1,0:T(2,128)(2,1)S(1)} %reshape.94), channel_id=1, replica_groups=mesh['date'=8,'pix'=4] {'date'}, dimensions={0} | all-to-all | bytes 720896 | tf_op jit(solution)/shard_map/all_to_all | solution.py:55
  37.7 10.2 %reshape.95 = bf16[2048,1,8,11]{3,2,1,0:T(8,128)(2,1)} reshape(bf16[8,2,11264]{2,1,0:T(2,128)(2,1)S(1)} %all_to_all.4) | data formatting | bytes 720896
  47.9 17.2 %copy.34 = f32[1,11,8,8,256]{2,4,3,1,0:T(8,128)} copy(bf16[1,11,8,8,256]{1,2,4,3,0:T(8,128)(2,1)} %bitcast.39) | data formatting | bytes 1081344 | tf_op jit(solution)/shard_map/convert_element_type | solution.py:55
  65.1 1.4 fusion.8
  66.5 1.0 reduce_sum.91
  67.6 0.1 copy.37
  67.6 5.6 %multiply_reduce_fusion.4 = f32[10,8,256]{1,2,0:T(8,128)S(1)} fusion(f32[8,11,8,256]{2,3,0,1:T(8,128)} %bitcast.27, f32[8,8,256]{1,2,0:T(8,128)S(1)} %get-tuple-element.10), kind=kLoop, calls=%fused_computation.4 | loop fusion | flops 307200 | bytes 802816 | tf_op jit(solution)/shard_map/reduce_sum | solution.py:36
  73.2 0.4 copy.38
  73.6 0.4 copy.39
  74.0 5.6 %multiply_reduce_fusion.3 = f32[8,8,256]{1,2,0:T(8,128)S(1)} fusion(f32[8,11,8,256]{2,3,0,1:T(8,128)} %bitcast.28, f32[10,8,256]{1,2,0:T(8,128)S(1)} %copy.39), kind=kLoop, calls=%fused_computation.3 | loop fusion | flops 475136 | bytes 802816 | tf_op jit(solution)/shard_map/reduce_sum | solution.py:35
  79.6 1.5 %multiply_reduce_fusion.6 = f32[8,256]{0,1:T(8,128)S(1)} fusion(f32[8,8,256]{1,2,0:T(8,128)S(1)} %multiply_reduce_fusion.3, f32[8,11,8,256]{2,3,0,1:T(8,128)} %bitcast.29), kind=kLoop, calls=%fused_computation.11 | loop fusion | flops 47104 | bytes 139264 | tf_op jit(solution)/shard_map/reduce_sum | solution.py:37
  81.0 1.5 %fusion.1 = f32[8,8,256]{1,2,0:T(8,128)S(1)} fusion(f32[8,8,256]{1,2,0:T(8,128)S(1)} %multiply_reduce_fusion.3, f32[8,11,8,256]{2,3,0,1:T(8,128)} %bitcast.30), kind=kLoop, calls=%fused_computation.8 | loop fusion | flops 32768 | bytes 196608 | tf_op jit(solution)/shard_map/mul | solution.py:36
  82.5 0.1 copy.42
  82.6 6.6 %multiply_reduce_fusion.2 = f32[10,8,256]{1,2,0:T(8,128)} fusion(f32[8,11,8,256]{2,3,0,1:T(8,128)} %bitcast.31, f32[8,8,256]{1,2,0:T(8,128)S(1)} %fusion.1), kind=kLoop, calls=%fused_computation.2 | loop fusion | flops 307200 | bytes 802816 | tf_op jit(solution)/shard_map/reduce_sum | solution.py:36
  89.2 0.0 slice-start
  89.2 1.8 %copy.41 = f32[10,8,256]{2,1,0:T(8,128)S(1)} copy(f32[10,8,256]{1,2,0:T(8,128)} %multiply_reduce_fusion.2) | data formatting | bytes 163840 | tf_op jit(solution)/shard_map/reduce_sum | solution.py:36
  91.1 1.5 %copy.43 = f32[10,8,256]{1,2,0:T(8,128)} copy(f32[10,8,256]{2,1,0:T(8,128)S(1)} %add_divide_fusion.1) | data formatting | bytes 163840 | tf_op jit(solution)/shard_map/div | solution.py:38
  92.6 0.0 slice-start.1
  92.6 0.0 slice-start.2
  92.6 6.1 %multiply_reduce_fusion.1 = f32[8,8,256]{1,2,0:T(8,128)S(1)} fusion(f32[8,11,8,256]{2,3,0,1:T(8,128)} %bitcast.32, f32[10,8,256]{1,2,0:T(8,128)} %copy.43), kind=kLoop, calls=%fused_computation.1 | loop fusion | flops 475136 | bytes 802816 | tf_op jit(solution)/shard_map/reduce_sum | solution.py:35
  98.7 1.5 %multiply_reduce_fusion.5 = f32[8,256]{0,1:T(8,128)S(1)} fusion(f32[8,8,256]{1,2,0:T(8,128)S(1)} %multiply_reduce_fusion.1, f32[8,11,8,256]{2,3,0,1:T(8,128)} %bitcast.33), kind=kLoop, calls=%fused_computation.9 | loop fusion | flops 47104 | bytes 139264 | tf_op jit(solution)/shard_map/reduce_sum | solution.py:37
  100.1 1.5 %fusion = f32[8,8,256]{1,2,0:T(8,128)S(1)} fusion(f32[8,8,256]{1,2,0:T(8,128)S(1)} %multiply_reduce_fusion.1, f32[8,11,8,256]{2,3,0,1:T(8,128)} %bitcast.34), kind=kLoop, calls=%fused_computation.6 | loop fusion | flops 32768 | bytes 196608 | tf_op jit(solution)/shard_map/mul | solution.py:36
  101.6 0.0 slice-done
  101.6 0.0 slice-done.1
  101.6 0.0 slice-done.2
  101.6 2.5 %multiply_reduce_fusion = f32[10,8,256]{1,2,0:T(8,128)} fusion(f32[8,11,8,256]{2,3,0,1:T(8,128)S(1)} %bitcast.37, f32[8,8,256]{1,2,0:T(8,128)S(1)} %fusion), kind=kLoop, calls=%fused_computation | loop fusion | flops 307200 | bytes 802816 | tf_op jit(solution)/shard_map/reduce_sum | solution.py:36
  104.1 1.7 %copy.45 = f32[10,8,256]{2,1,0:T(8,128)S(1)} copy(f32[10,8,256]{1,2,0:T(8,128)} %multiply_reduce_fusion) | data formatting | bytes 163840 | tf_op jit(solution)/shard_map/reduce_sum | solution.py:36
  105.8 0.1 copy.46
  105.9 32.0 %all_gather.3 = f32[10,8,2048]{2,1,0:T(8,128)S(1)} all-gather(f32[10,8,256]{2,1,0:T(8,128)S(1)} %add_divide_fusion), channel_id=1, replica_groups=mesh['date'=8,'pix'=4] {'date'}, dimensions={2}, use_global_device_ids=true | all-gather | bytes 737280 | tf_op jit(solution)/shard_map/all_gather | solution.py:57
  137.9 0.2 fusion.7
  138.1 5.7 %all-reduce.1 = (f32[10]{0:T(128)S(1)}, f32[10]{0:T(128)S(1)}) all-reduce(f32[10]{0:T(128)S(1)} %get-tuple-element.6, f32[10]{0:T(128)S(1)} %get-tuple-element.5), channel_id=1, replica_groups=mesh['date'=8,'pix'=4] {'pix'}, use_global_device_ids=true, to_apply=%region_11.12 | all-reduce | flops 20 | bytes 160 | tf_op jit(solution)/shard_map/psum | solution.py:59
  143.7 1.0 subtract_divide_fusion
  (10 shorter events, 0.2 us)
Async XLA Ops:
  0.9 3.7 %collective-permute-start = (bf16[1,1,2048]{2,1,0:T(2,128)(2,1)S(1)}, bf16[1,1,2048]{2,1,0:T(2,128)(2,1)S(1)}, u32[]{:S(2)}, u32[]{:S(2)}) collective-permute-start(bf16[1,1,2048]{2,1,0:T(2,128)(2,1)S(1)} %get-tuple-element.11), channel_id=1, source_target_pairs={{0,1},{1,2},{2,3},{4,5},{5,6},{6,7},{8,9},{9,10},{10,11},{12,13},{... | collective-permute-start | bytes 12296 | tf_op jit(solution)/shard_map/ppermute | solution.py:20
  3.3 5.2 %collective-permute-start.1 = (bf16[1,1,2048]{2,1,0:T(2,128)(2,1)S(1)}, bf16[1,1,2048]{2,1,0:T(2,128)(2,1)S(1)}, u32[]{:S(2)}, u32[]{:S(2)}) collective-permute-start(bf16[1,1,2048]{2,1,0:T(2,128)(2,1)S(1)} %get-tuple-element.12), channel_id=1, source_target_pairs={{1,0},{2,1},{3,2},{5,4},{6,5},{7,6},{9,8},{10,9},{11,10},{13,12},{... | collective-permute-start | bytes 12296 | tf_op jit(solution)/shard_map/ppermute | solution.py:22
  89.2 12.4 %slice-start = ((s8[11534336]{0:T(1024)(128)(4,1)}), s8[3145728]{0:T(1024)(128)(4,1)S(1)}, s32[]{:S(2)}) async-start(s8[11534336]{0:T(1024)(128)(4,1)} %bitcast.35), calls=%async_computation.1 | async-start | bytes 6291456
  92.6 9.1 %slice-start.1 = ((s8[11534336]{0:T(1024)(128)(4,1)}), s8[4194304]{0:T(1024)(128)(4,1)S(1)}, s32[]{:S(2)}) async-start(s8[11534336]{0:T(1024)(128)(4,1)} %bitcast.35), calls=%async_computation.2 | async-start | bytes 8388608
  92.6 9.1 %slice-start.2 = ((s8[11534336]{0:T(1024)(128)(4,1)}), s8[4194304]{0:T(1024)(128)(4,1)S(1)}, s32[]{:S(2)}) async-start(s8[11534336]{0:T(1024)(128)(4,1)} %bitcast.35), calls=%async_computation.3 | async-start | bytes 8388608
